TPU v7x, 32 devices: a whole 2x2x4 slice. The times are simulated.
32 devices in a mesh: part: 2 (over x), tpa: 4 (over z), tpb: 4 (over y, core).
Axes of the slice: x: 2, y: 2, z: 4, core: 2. Of those that a mesh axis runs over, the one named last changes fastest.
Arguments:
- x: bfloat16 [16, 2048, 2048], P(('part', 'tpb')), parts along dimension 0
- lengths: int32 [16], P(('part', 'tpb')), parts along dimension 0
- k_buf: bfloat16 [16, 2048, 8, 64], P(('part', 'tpb'), None, 'tpa'), parts along dimension 0
- v_buf: bfloat16 [16, 2048, 8, 64], P(('part', 'tpb'), None, 'tpa'), parts along dimension 0
- w_qkv: bfloat16 [4096, 3072], P('part', ('tpa', 'tpb')), parts along dimension 0
- w_o: bfloat16 [4096, 2048], P(('part', 'tpa', 'tpb')), parts along dimension 0
- w_gate_up: bfloat16 [4096, 16384], P('part', ('tpa', 'tpb')), parts along dimension 0
- w_down: bfloat16 [16384, 2048], P(('part', 'tpa', 'tpb')), parts along dimension 0
- g_attn: bfloat16 [4096], P('part'), parts along dimension 0
- g_mlp: bfloat16 [4096], P('part'), parts along dimension 0
Outputs:
- output 1: bfloat16 [16, 2048, 2048], P(('part', 'tpb')), parts along dimension 0
- output 2: bfloat16 [16, 2048, 8, 64], P(('part', 'tpb'), None, 'tpa'), parts along dimension 0
- output 3: bfloat16 [16, 2048, 8, 64], P(('part', 'tpb'), None, 'tpa'), parts along dimension 0
- output 4: bfloat16 [4096, 2048], P('part', 'tpa'), parts along dimension 0
- output 5: bfloat16 [4096, 512], P('part', 'tpa'), parts along dimension 0
- output 6: bfloat16 [4096, 512], P('part', 'tpa'), parts along dimension 0
- output 7: bfloat16 [4096, 2048], P(('part', 'tpa')), parts along dimension 0
- output 8: bfloat16 [4096, 8192], P('part', 'tpa'), parts along dimension 0
- output 9: bfloat16 [4096, 8192], P('part', 'tpa'), parts along dimension 0
- output 10: bfloat16 [16384, 2048], P(('part', 'tpa')), parts along dimension 0
There are 2 independent parts. A program takes and returns all parts, laid end to end along the dimension named above; each array names one.
All inputs are finite; a program needn't handle non-finite values.
Results may differ from a plain program's by a relative error of at most 0.0141267.
Values are sent between devices in bfloat16 or wider.
A program may use at most 1 GiB of HBM per device.

v0:
```python
import functools
import math
import jax
import jax.numpy as jnp
from jax import lax
from jax.sharding import PartitionSpec as P
from jax.experimental import pallas as pl
from jax.experimental.pallas import tpu as pltpu

ROPE_BASE = 500000.0
ROPE_FACTOR = 8.0
LOW_FREQ = 1.0
HIGH_FREQ = 4.0
ORIG_CONTEXT = 8192.0
NORM_EPS = 1e-5
MASK_VALUE = -1e30
HEAD = 64
LANES = 128

FAR_ROW = [(0, 2), (2, 0), (1, 3), (3, 1)]
NEAR_ROW = [(0, 1), (1, 0), (2, 3), (3, 2)]
OTHER_CHIP = [(0, 2), (2, 0), (1, 3), (3, 1)]
OTHER_CORE = [(0, 1), (1, 0), (2, 3), (3, 2)]


def rms_norm(x_in, gain_vec):
    x_wide = x_in.astype(jnp.float32)
    mean_sq = jnp.mean(x_wide * x_wide, axis=-1, keepdims=True)
    return (x_wide * lax.rsqrt(mean_sq + NORM_EPS) * gain_vec.astype(jnp.float32)).astype(jnp.bfloat16)


def rope_tables(seq_len, head_dim):
    exponent = jnp.arange(head_dim // 2, dtype=jnp.float32) * (2.0 / head_dim)
    inv_freq = 1.0 / jnp.power(ROPE_BASE, exponent)
    wavelen = 2.0 * math.pi / inv_freq
    smooth = (ORIG_CONTEXT / wavelen - LOW_FREQ) / (HIGH_FREQ - LOW_FREQ)
    blended = (1.0 - smooth) * inv_freq / ROPE_FACTOR + smooth * inv_freq
    rope_freq = jnp.where(wavelen < ORIG_CONTEXT / HIGH_FREQ, inv_freq, jnp.where(wavelen > ORIG_CONTEXT / LOW_FREQ, inv_freq / ROPE_FACTOR, blended))
    angles = jnp.arange(seq_len, dtype=jnp.float32)[:, None] * rope_freq[None, :]
    return jnp.cos(angles), jnp.sin(angles)


def apply_rope(vec_in, cos_tab, sin_tab):
    half_dim = vec_in.shape[-1] // 2
    first_half = vec_in[..., :half_dim]
    second_half = vec_in[..., half_dim:]
    return jnp.concatenate([first_half * cos_tab - second_half * sin_tab, second_half * cos_tab + first_half * sin_tab], axis=-1)


def attn_kernel(tile, q_ref, kv_ref, cos_ref, sin_ref, aug_ref, o_ref, qe_s, qo_s, k_s, ve_s, vo_s):
    seq = q_ref.shape[0]
    lane = lax.broadcasted_iota(jnp.int32, (tile, LANES), 1)
    low = lane < HEAD
    first = lax.rem(lane, HEAD) < HEAD // 2
    ones = jnp.ones((tile, LANES), jnp.float32)
    hot = jnp.where(lane == HEAD, 1.0, 0.0)

    def rope(val, cos, sin):
        rot = jnp.where(first, pltpu.roll(val, LANES - HEAD // 2, 1), pltpu.roll(val, HEAD // 2, 1))
        return val * cos + rot * sin

    for i in range(seq // tile):
        rows = slice(i * tile, (i + 1) * tile)
        cos, sin = cos_ref[rows, :], sin_ref[rows, :]
        q = rope(q_ref[rows, :].astype(jnp.float32), cos, sin).astype(jnp.bfloat16).astype(jnp.float32) * HEAD ** -0.5
        qe_s[rows, :] = jnp.where(low, q, hot).astype(jnp.bfloat16)
        qo_s[rows, :] = jnp.where(low, pltpu.roll(q, HEAD, 1), hot).astype(jnp.bfloat16)
        kv = kv_ref[rows, :].astype(jnp.float32)
        k_s[rows, :] = jnp.where(low, rope(kv, cos, sin), aug_ref[rows, :].astype(jnp.float32)).astype(jnp.bfloat16)
        ve_s[rows, :] = jnp.where(low, pltpu.roll(kv, HEAD, 1), ones).astype(jnp.bfloat16)
        vo_s[rows, :] = jnp.where(low, ones, kv).astype(jnp.bfloat16)
    causal = lax.broadcasted_iota(jnp.int32, (tile, tile), 1) <= lax.broadcasted_iota(jnp.int32, (tile, tile), 0)
    dims = (((1,), (1,)), ((), ()))
    for i in range(seq // tile):
        rows = slice(i * tile, (i + 1) * tile)
        outs = []
        for qs, vs in ((qe_s, ve_s), (qo_s, vo_s)):
            q = qs[rows, :]
            diag = jnp.where(causal, lax.dot_general(q, k_s[rows, :], dims, preferred_element_type=jnp.float32), MASK_VALUE)
            top = jnp.max(diag, axis=1, keepdims=True)
            if i:
                past = lax.dot_general(q, k_s[:i * tile, :], dims, preferred_element_type=jnp.float32)
                top = jnp.maximum(top, jnp.max(past, axis=1, keepdims=True))
            out = jnp.dot(jnp.exp(diag - top).astype(jnp.bfloat16), vs[rows, :], preferred_element_type=jnp.float32)
            if i:
                out = out + jnp.dot(jnp.exp(past - top).astype(jnp.bfloat16), vs[:i * tile, :], preferred_element_type=jnp.float32)
            outs.append(out)
        num = jnp.where(low, outs[0], outs[1])
        den = pltpu.roll(jnp.where(low, outs[1], outs[0]), HEAD, 1)
        o_ref[rows, :] = (num / den).astype(jnp.bfloat16)


def attention(qkv, cos, sin, aug, prompt):
    cols = qkv.shape[1]
    seq = cos.shape[0]
    groups = cols // (3 * LANES)
    tile = min(512, seq)

    def block(index):
        return pl.BlockSpec((seq, LANES), index)

    return pl.pallas_call(
        functools.partial(attn_kernel, tile),
        grid=(groups, 2),
        in_specs=[block(lambda g, p: (prompt, 3 * g + p)), block(lambda g, p: (prompt, 3 * g + 2)), block(lambda g, p: (0, 0)), block(lambda g, p: (0, 0)), block(lambda g, p: (prompt, 0))],
        out_specs=block(lambda g, p: (0, 2 * g + p)),
        out_shape=jax.ShapeDtypeStruct((seq, groups * 2 * LANES), jnp.bfloat16),
        scratch_shapes=[pltpu.VMEM((seq, LANES), jnp.bfloat16)] * 5,
        cost_estimate=pl.CostEstimate(flops=groups * 16 * seq * seq * LANES, bytes_accessed=seq * groups * 2560, transcendentals=groups * 2 * seq * seq),
        name="attention",
    )(qkv, qkv, cos, sin, aug)


def place_kernel(base_ref, *refs):
    outs = refs[4:]
    width = outs[0].shape[1]
    for k in range(4):
        @pl.when(pl.program_id(0) == k)
        def _(k=k):
            for n, out in enumerate(outs):
                out[...] = refs[k][:, n * width:(n + 1) * width]


def place(srcs, base, count, by_rows):
    rows, cols = srcs[0].shape
    width = cols // count
    tile = min(512, rows)
    steps = rows // tile

    def source(k):
        return pl.BlockSpec((tile, cols), lambda r, i, base: (jnp.where(r == k, i, jnp.where(r < k, 0, steps - 1)), 0))

    def target(r, i, base):
        spot = base[0] ^ r
        return (spot * steps + i, 0) if by_rows else (i, spot)

    shape = (4 * rows, width) if by_rows else (rows, 4 * width)
    return pl.pallas_call(
        place_kernel,
        grid_spec=pltpu.PrefetchScalarGridSpec(num_scalar_prefetch=1, grid=(4, steps), in_specs=[source(k) for k in range(4)], out_specs=[pl.BlockSpec((tile, width), target)] * count),
        out_shape=[jax.ShapeDtypeStruct(shape, srcs[0].dtype)] * count,
        cost_estimate=pl.CostEstimate(flops=4 * rows * cols * 512, bytes_accessed=16 * rows * cols, transcendentals=0),
        name="place",
    )(base.reshape(1).astype(jnp.int32), *srcs)


def mlp_kernel(chunk, batch, *refs):
    x_ref, *refs = refs
    heads_refs, refs = refs[:4 * batch], refs[4 * batch:]
    (wo_ref, ga_ref, gb_ref, gc_ref, gd_ref, da_ref, db_ref, dc_ref, dd_ref, gain_ref,
     y_ref, land_in, land_across,
     wo_v, gu_v, down_v, x_v, o_v, h_v, u_v, acc_v, part_v, half_v, stage_v, y_v,
     w_sem, in_sem, stage_sem, in_send, in_recv, ac_send, ac_recv, out_send, out_recv, y_sem, tail_sem) = refs
    rows_all, _ = x_ref.shape
    count = rows_all // chunk
    heads = heads_refs[0].shape[1]
    per_prompt = count // batch
    last = count - 1
    half_rows = chunk // 2
    ff = da_ref.shape[0]
    part_id = lax.axis_index('part')
    z = lax.axis_index('tpa')
    tpb = lax.axis_index('tpb')
    is_end = (z == 0) | (z == 3)
    is_mid = (z == 1) | (z == 2)

    def device(row):
        return (part_id, row, tpb)

    mesh_ids = pl.DeviceIdType.MESH
    inner = 1 + z // 2
    other = 3 - z
    outer = 3 * (z // 2)
    barrier = pltpu.get_barrier_semaphore()

    @pl.when(is_end)
    def _():
        pl.semaphore_signal(barrier, 1, device_id=device(inner), device_id_type=mesh_ids)
        pl.semaphore_wait(barrier, 1)

    @pl.when(is_mid)
    def _():
        pl.semaphore_signal(barrier, 1, device_id=device(outer), device_id_type=mesh_ids)
        pl.semaphore_signal(barrier, 1, device_id=device(other), device_id_type=mesh_ids)
        pl.semaphore_wait(barrier, 2)

    near = z + 1 - 2 * (z % 2)
    far = (z + 2) % 4
    both = far + 1 - 2 * (far % 2)
    spots = (z, near, far, both)

    def rows_of(k):
        return pl.ds(pl.multiple_of(k * chunk, chunk), chunk)

    def input_copies(k, prompt):
        slot = k % 2
        copies = [pltpu.make_async_copy(x_ref.at[rows_of(k)], x_v.at[slot], in_sem.at[slot, 4])]
        for n, spot in enumerate(spots):
            cols = pl.ds(pl.multiple_of(spot * heads, heads), heads)
            copies.append(pltpu.make_async_copy(heads_refs[4 * prompt + n].at[rows_of(k % per_prompt)], o_v.at[slot, :, cols], in_sem.at[slot, n]))
        return copies

    def start_inputs(k):
        for prompt in range(batch):
            @pl.when(k // per_prompt == prompt)
            def _(prompt=prompt):
                for copy in input_copies(k, prompt):
                    copy.start()

    weights = [pltpu.make_async_copy(wo_ref, wo_v, w_sem.at[8])]
    for n, (g_ref, d_ref) in enumerate(((ga_ref, da_ref), (gb_ref, db_ref), (gc_ref, dc_ref), (gd_ref, dd_ref))):
        weights.append(pltpu.make_async_copy(g_ref, gu_v.at[n], w_sem.at[2 * n]))
        weights.append(pltpu.make_async_copy(d_ref, down_v.at[n], w_sem.at[2 * n + 1]))
    for copy in input_copies(0, 0) + weights:
        copy.start()

    def send_in(k):
        return pltpu.make_async_remote_copy(src_ref=part_v.at[k % 3], dst_ref=land_in.at[rows_of(k)], send_sem=in_send.at[k], recv_sem=in_recv.at[k], device_id=device(inner), device_id_type=mesh_ids)

    def send_across(k):
        return pltpu.make_async_remote_copy(src_ref=half_v.at[k % 3], dst_ref=land_across.at[rows_of(k)], send_sem=ac_send.at[k], recv_sem=ac_recv.at[k], device_id=device(other), device_id_type=mesh_ids)

    def send_out(k):
        return pltpu.make_async_remote_copy(src_ref=y_v.at[k % 2], dst_ref=y_ref.at[rows_of(k)], send_sem=out_send.at[k], recv_sem=out_recv.at[k], device_id=device(outer), device_id_type=mesh_ids)

    def keep_out(k):
        return pltpu.make_async_copy(y_v.at[k % 2], y_ref.at[rows_of(k)], y_sem.at[k % 2])

    def tail(ref, n):
        return ref.at[pl.ds(last * chunk + n * half_rows, half_rows)]

    def tail_copy(src, dst, row, which, n):
        return pltpu.make_async_remote_copy(src_ref=src.at[:, pl.ds(n * half_rows, half_rows)].at[0], dst_ref=tail(dst, n), send_sem=tail_sem.at[which, n], recv_sem=tail_sem.at[which + 1, n], device_id=device(row), device_id_type=mesh_ids)

    def tail_in(n):
        return tail_copy(part_v.at[pl.ds(last % 3, 1)], land_in, inner, 0, n)

    def tail_across(n):
        return tail_copy(half_v.at[pl.ds(last % 3, 1)], land_across, other, 2, n)

    def tail_out(n):
        return tail_copy(y_v.at[pl.ds(last % 2, 1)], y_ref, outer, 4, n)

    def tail_keep(n):
        return pltpu.make_async_copy(y_v.at[last % 2, pl.ds(n * half_rows, half_rows)], tail(y_ref, n), tail_sem.at[6, n])

    def tail_fetch(ref, slot, n):
        return pltpu.make_async_copy(tail(ref, n), stage_v.at[slot, pl.ds(n * half_rows, half_rows)], tail_sem.at[7, n])

    def fetch(ref, k, slot):
        return pltpu.make_async_copy(ref.at[rows_of(k)], stage_v.at[slot], stage_sem.at[slot])

    def step(k, carry):
        @pl.when(k < count)
        def _():
            for copy in input_copies(k, 0):
                copy.wait()

            @pl.when(k + 1 < count)
            def _():
                start_inputs(k + 1)

            @pl.when(k == 0)
            def _():
                weights[0].wait()

            @pl.when(is_end & (k >= 3))
            def _():
                send_in(k - 3).wait_send()

            slot = k % 2
            hidden = (x_v[slot].astype(jnp.float32) + jnp.dot(o_v[slot], wo_v[...], preferred_element_type=jnp.float32)).astype(jnp.bfloat16)
            h_v[k % 3] = hidden
            wide = hidden.astype(jnp.float32)
            mean_sq = jnp.mean(wide * wide, axis=1, keepdims=True)
            u_v[...] = (wide * lax.rsqrt(mean_sq + NORM_EPS) * gain_ref[...].astype(jnp.float32)).astype(jnp.bfloat16)
            acc_v[...] = jnp.zeros_like(acc_v)

            def ff_block(r, inner_carry):
                @pl.when(k == 0)
                def _():
                    pltpu.make_async_copy(ga_ref, gu_v.at[r], w_sem.at[2 * r]).wait()
                    pltpu.make_async_copy(da_ref, down_v.at[r], w_sem.at[2 * r + 1]).wait()

                gate_up = jnp.dot(u_v[...], gu_v[r], preferred_element_type=jnp.float32)
                gate = gate_up[:, :ff].astype(jnp.bfloat16).astype(jnp.float32)
                up = gate_up[:, ff:].astype(jnp.bfloat16).astype(jnp.float32)
                mid = (jax.nn.silu(gate) * up).astype(jnp.bfloat16)
                acc_v[...] += jnp.dot(mid, down_v[r], preferred_element_type=jnp.float32)
                return inner_carry

            lax.fori_loop(0, 4, ff_block, 0)
            part_v[k % 3] = acc_v[...].astype(jnp.bfloat16)

            @pl.when(is_end & (k < last))
            def _():
                send_in(k).start()

            @pl.when(is_end & (k == last))
            def _():
                for n in range(2):
                    tail_in(n).start()

        @pl.when(is_mid & (k >= 1) & (k < count))
        def _():
            j = k - 1
            send_in(j).wait_recv()
            copy = fetch(land_in, j, 0)
            copy.start()

            @pl.when(j >= 3)
            def _():
                send_across(j - 3).wait_send()

            copy.wait()
            half_v[j % 3] = (part_v[j % 3].astype(jnp.float32) + stage_v[0].astype(jnp.float32)).astype(jnp.bfloat16)
            send_across(j).start()

        @pl.when(is_mid & (k == count))
        def _():
            send_across(last - 3).wait_send()
            for n in range(2):
                tail_in(n).wait_recv()
                copy = tail_fetch(land_in, 0, n)
                copy.start()
                copy.wait()
                rows = slice(n * half_rows, (n + 1) * half_rows)
                half_v[last % 3, rows, :] = (part_v[last % 3, rows, :].astype(jnp.float32) + stage_v[0, rows, :].astype(jnp.float32)).astype(jnp.bfloat16)
                tail_across(n).start()

        @pl.when(is_mid & (k >= 2) & (k <= count))
        def _():
            j = k - 2
            send_across(j).wait_recv()
            copy = fetch(land_across, j, 1)
            copy.start()

            @pl.when(j >= 2)
            def _():
                send_out(j - 2).wait_send()
                keep_out(j - 2).wait()

            copy.wait()
            total = half_v[j % 3].astype(jnp.float32) + stage_v[1].astype(jnp.float32)
            y_v[j % 2] = (h_v[j % 3].astype(jnp.float32) + total).astype(jnp.bfloat16)
            send_out(j).start()
            keep_out(j).start()

        @pl.when(is_mid & (k > count))
        def _():
            send_out(last - 2).wait_send()
            keep_out(last - 2).wait()
            for n in range(2):
                tail_across(n).wait_recv()
                copy = tail_fetch(land_across, 1, n)
                copy.start()
                copy.wait()
                rows = slice(n * half_rows, (n + 1) * half_rows)
                total = half_v[last % 3, rows, :].astype(jnp.float32) + stage_v[1, rows, :].astype(jnp.float32)
                y_v[last % 2, rows, :] = (h_v[last % 3, rows, :].astype(jnp.float32) + total).astype(jnp.bfloat16)
                tail_out(n).start()
                tail_keep(n).start()

        return carry

    lax.fori_loop(0, count + 2, step, 0)

    @pl.when(is_end)
    def _():
        for k in range(count - 3, last):
            send_in(k).wait_send()

        def arrive(k, carry):
            send_out(k).wait_recv()
            return carry

        lax.fori_loop(0, last, arrive, 0)
        for n in range(2):
            tail_in(n).wait_send()
            tail_out(n).wait_recv()

    @pl.when(is_mid)
    def _():
        for k in range(count - 3, last):
            send_across(k).wait_send()
        send_out(last - 1).wait_send()
        keep_out(last - 1).wait()
        for n in range(2):
            tail_across(n).wait_send()
            tail_out(n).wait_send()
            tail_keep(n).wait()


def mlp(x_flat, heads, w_o_all, gu, down, gain, chunk, batch):
    rows, dim = x_flat.shape
    count = rows // chunk
    ff = down[0].shape[0]
    anywhere = pl.BlockSpec(memory_space=pl.ANY)
    whole = jax.ShapeDtypeStruct((rows, dim), jnp.bfloat16)
    inner = w_o_all.shape[0]
    dma = pltpu.SemaphoreType.DMA
    out = pl.pallas_call(
        functools.partial(mlp_kernel, chunk, batch),
        in_specs=[anywhere] * (10 + 4 * batch) + [pl.BlockSpec(memory_space=pltpu.VMEM)],
        out_specs=[anywhere] * 3,
        out_shape=[whole] * 3,
        scratch_shapes=[
            pltpu.VMEM((inner, dim), jnp.bfloat16), pltpu.VMEM((4, dim, 2 * ff), jnp.bfloat16), pltpu.VMEM((4, ff, dim), jnp.bfloat16),
            pltpu.VMEM((2, chunk, dim), jnp.bfloat16), pltpu.VMEM((2, chunk, inner), jnp.bfloat16), pltpu.VMEM((3, chunk, dim), jnp.bfloat16),
            pltpu.VMEM((chunk, dim), jnp.bfloat16), pltpu.VMEM((chunk, dim), jnp.float32), pltpu.VMEM((3, chunk, dim), jnp.bfloat16),
            pltpu.VMEM((3, chunk, dim), jnp.bfloat16), pltpu.VMEM((2, chunk, dim), jnp.bfloat16), pltpu.VMEM((2, chunk, dim), jnp.bfloat16),
            dma((9,)), dma((2, 5)), dma((2,)), dma((count,)), dma((count,)), dma((count,)), dma((count,)), dma((count,)), dma((count,)), dma((2,)), dma((8, 2)),
        ],
        compiler_params=pltpu.CompilerParams(collective_id=1, has_side_effects=True, vmem_limit_bytes=63 * 1024 * 1024),
        cost_estimate=pl.CostEstimate(flops=2 * rows * dim * (inner + 12 * ff), bytes_accessed=8 * rows * dim, transcendentals=4 * rows * ff),
        name="mlp",
    )(x_flat, *heads, w_o_all, *gu, *down, gain.reshape(1, dim))
    return out[0]


def with_other_core(block, chip):
    return block, lax.ppermute(block, 'tpb', OTHER_CORE), chip, lax.ppermute(chip, 'tpb', OTHER_CORE)


def dot(a, b):
    return jnp.dot(a, b, preferred_element_type=jnp.float32)


def layer(x_loc, len_loc, k_buf, v_buf, w_qkv, w_o, w_gate_up, w_down, g_attn, g_mlp):
    batch, seq, model_dim = x_loc.shape
    tpa = lax.axis_index('tpa')
    tpb = lax.axis_index('tpb')
    x_flat = x_loc.reshape(batch * seq, model_dim)

    qkv_own = lax.all_gather(w_qkv, 'tpb', axis=1, tiled=True)
    far = lax.ppermute(w_qkv, 'tpa', FAR_ROW)
    normed = rms_norm(x_flat, g_attn)
    act_own = dot(normed, qkv_own).astype(jnp.bfloat16)
    act_own, far = lax.optimization_barrier((act_own, far))
    qkv_far = lax.all_gather(far, 'tpb', axis=1, tiled=True)
    w_o_all = lax.all_gather(w_o, ('tpa', 'tpb'), axis=0, tiled=True)
    w_gate_up, w_down, _ = lax.optimization_barrier((w_gate_up, w_down, qkv_own))
    cos_tab, sin_tab = rope_tables(seq, HEAD)
    cos_wide = jnp.tile(cos_tab, (1, 4))
    sin_wide = jnp.tile(jnp.concatenate([-sin_tab, sin_tab], axis=1), (1, 2))
    positions = jnp.arange(seq)
    at_mask = (jnp.arange(LANES) == HEAD)[None, None, :] & (positions[None, :, None] >= len_loc[:, None, None])
    aug = jnp.where(at_mask, MASK_VALUE, 0.0).astype(jnp.bfloat16)

    aug = aug.reshape(batch * seq, LANES)
    act_far = dot(normed, qkv_far).astype(jnp.bfloat16)
    heads_own = [attention(act_own, cos_wide, sin_wide, aug, b) for b in range(batch)]
    heads_far = []
    for b in range(batch):
        heads_far.append(attention(act_far, cos_wide, sin_wide, aug, b))
    gu_chip = lax.ppermute(w_gate_up, 'tpb', OTHER_CHIP)
    down_chip = lax.ppermute(w_down, 'tpb', OTHER_CHIP)
    near_own = [lax.ppermute(h, 'tpa', NEAR_ROW) for h in heads_own]
    near_far = []
    for b in range(batch):
        near_far.append(lax.ppermute(heads_far[b], 'tpa', NEAR_ROW))
    _, gu_chip = lax.optimization_barrier((heads_far[0], gu_chip))
    _, down_chip = lax.optimization_barrier((heads_far[-1], down_chip))
    gu = with_other_core(w_gate_up, gu_chip)
    down = with_other_core(w_down, down_chip)
    w_gate, w_up = place(gu, tpb, 2, False)
    w_down_gen, = place(down, tpb, 1, True)

    heads = []
    for b in range(batch):
        heads += [heads_own[b], near_own[b], heads_far[b], near_far[b]]
    o_rows = w_o_all.shape[0] // 4
    w_o_gen = lax.dynamic_slice(w_o_all, (tpa * o_rows, 0), (o_rows, w_o_all.shape[1]))
    heads[-1], w_o_gen = lax.optimization_barrier((heads[-1], w_o_gen))
    layer_out = mlp(x_flat, heads, w_o_all, gu, down, g_mlp, min(256, seq // 8), batch).reshape(batch, seq, model_dim)

    kv_local = k_buf.shape[2]
    width = act_own.shape[1] // kv_local
    q_width = width - 2 * HEAD

    def columns(array, begin, size):
        return [array[..., g * width + begin:g * width + begin + size] for g in range(kv_local)]

    act_seq = act_own.reshape(batch, seq, -1)
    k_new = jnp.stack(columns(act_seq, q_width, HEAD), axis=2)
    values = jnp.stack(columns(act_seq, q_width + HEAD, HEAD), axis=2)
    k_rot = apply_rope(k_new.astype(jnp.float32), cos_tab[:, None, :], sin_tab[:, None, :]).astype(jnp.bfloat16)
    valid = (positions[None, :] < len_loc[:, None])[:, :, None, None]
    k_cache = jnp.where(valid, k_rot, k_buf)
    v_cache = jnp.where(valid, values, v_buf)

    w_query = jnp.concatenate(columns(qkv_own, 0, q_width), axis=1)
    w_key = jnp.concatenate(columns(qkv_own, q_width, HEAD), axis=1)
    w_value = jnp.concatenate(columns(qkv_own, q_width + HEAD, HEAD), axis=1)
    return (layer_out, k_cache, v_cache, w_query, w_key, w_value, w_o_gen, w_gate, w_up, w_down_gen)


def solution(mesh):
    batch_spec = P(('part', 'tpb'), None, None)
    len_spec = P(('part', 'tpb'))
    cache_spec = P(('part', 'tpb'), None, 'tpa', None)
    train_cols = P('part', ('tpa', 'tpb'))
    train_rows = P(('part', 'tpa', 'tpb'), None)
    gain_spec = P('part')
    gen_cols = P('part', 'tpa')
    gen_rows = P(('part', 'tpa'), None)
    return jax.shard_map(layer, mesh=mesh, in_specs=(batch_spec, len_spec, cache_spec, cache_spec, train_cols, train_rows, train_cols, train_rows, gain_spec, gain_spec), out_specs=(batch_spec, cache_spec, cache_spec, gen_cols, gen_cols, gen_cols, gen_rows, gen_cols, gen_cols, gen_rows), check_vma=False)
```

profile of v0, /device:TPU:0, one launch (start us, length us, event | category | flops | bytes accessed | tf_op | source)
XLA Modules:
  0.0 889.5 jit_solution(6898632712724387555)
XLA Ops:
  7.2 0.7 all-gather.4.cloned.1.call-update
  8.0 4.1 collective-permute-start
  12.1 7.3 multiply_reduce_fusion
  19.5 21.4 %all-gather.4.cloned.1.call-done = bf16[2048,768]{0,1:T(8,128)(2,1)} async-done(((bf16[2048,192]{0,1:T(8,128)(2,1)}), bf16[2048,768]{0,1:T(8,128)(2,1)}) %all-gather.4.cloned.1.call-update) | async-done | bytes 3145744 | tf_op jit(solution)/shard_map/all_gather | solution.py:435
  40.8 20.0 %convolution_convert_fusion.1.q_ref.kv_ref = bf16[4096,768]{1,0:T(8,128)(2,1)} fusion(bf16[2048,768]{0,1:T(8,128)(2,1)} %all-gather.4.cloned.1.call-done, bf16[4096,2048]{1,0:T(8,128)(2,1)} %bitcast.15, f32[2048]{0:T(1024)S(1)} %convert_element_type.28, f32[4096]{0:T(1024)S(1)} %bitcast.26), kind=kOutput, calls=%fused_computation.3 | convolution fusion | flops 12921602048 | bytes 26238976 | tf_op jit(solution)/shard_map/dot_general | solution.py:426
  60.8 0.9 copy-done.8
  61.8 0.7 all-gather.8.cloned.1.call-update
  62.5 1.0 fusion.2
  63.5 0.7 copy-done
  64.4 1.3 copy.41.sin_ref
  65.8 1.3 copy.40.cos_ref
  67.3 0.6 reshape.170.refs_18_
  67.9 3.1 select_convert_fusion.aug_ref
  70.9 0.3 collective-permute-start.6
  71.3 1.7 collective-permute-start.9
  73.0 0.2 collective-permute-start.8
  73.2 37.2 %attention.6.refs_5_ = bf16[2048,512]{1,0:T(8,128)(2,1)} custom-call(bf16[4096,768]{1,0:T(8,128)(2,1)} %convolution_convert_fusion.1.q_ref.kv_ref, bf16[4096,768]{1,0:T(8,128)(2,1)} %convolution_convert_fusion.1.q_ref.kv_ref, f32[2048,128]{1,0:T(8,128)} %copy.40.cos_ref, f32[2048,128]{1,0:T(8,128)} %copy.41.sin_ref, bf16[4096,128]{1,0:T(8,128)(2,1)} %select_convert_fusion.aug_ref), custom_call_target="tpu_custom_call" | custom-call | flops 17179869184 | bytes 10485760 | tf_op jit(solution)/shard_map/attention/pallas_call | solution.py:102
  110.4 1.5 collective-permute-start.3
  111.9 4.0 fusion.3
  115.8 2.5 copy.55
  118.3 1.1 copy.56
  119.5 1.1 copy.57
  120.6 1.1 copy.58
  121.7 1.3 fusion.4
  123.0 2.7 fusion.5
  125.7 20.4 %convolution_convert_fusion.q_ref.kv_ref = bf16[4096,768]{1,0:T(8,128)(2,1)} fusion(bf16[2048,768]{0,1:T(8,128)(2,1)} %all-gather.6.cloned.1.call-done, bf16[4096,2048]{1,0:T(8,128)(2,1)} %bitcast.16, f32[2048]{0:T(1024)S(1)} %convert_element_type.28, f32[4096]{0:T(1024)S(1)} %bitcast.27), kind=kOutput, calls=%fused_computation.2 | convolution fusion | flops 12921602048 | bytes 26238976 | tf_op jit(solution)/shard_map/dot_general | solution.py:426
  146.1 37.3 %attention.5.refs_3_ = bf16[2048,512]{1,0:T(8,128)(2,1)} custom-call(bf16[4096,768]{1,0:T(8,128)(2,1)} %convolution_convert_fusion.q_ref.kv_ref, bf16[4096,768]{1,0:T(8,128)(2,1)} %convolution_convert_fusion.q_ref.kv_ref, f32[2048,128]{1,0:T(8,128)} %copy.40.cos_ref, f32[2048,128]{1,0:T(8,128)} %copy.41.sin_ref, bf16[4096,128]{1,0:T(8,128)(2,1)} %select_convert_fusion.aug_ref), custom_call_target="tpu_custom_call" | custom-call | flops 17179869184 | bytes 10485760 | tf_op jit(solution)/shard_map/attention/pallas_call | solution.py:102
  183.4 23.7 %collective-permute-done.6.refs_12_.refs_2_ = bf16[2048,1024]{1,0:T(8,128)(2,1)} collective-permute-done((bf16[2048,1024]{1,0:T(8,128)(2,1)}, bf16[2048,1024]{1,0:T(8,128)(2,1)}, u32[]{:S(2)}, u32[]{:S(2)}) %collective-permute-start.6) | collective-permute-done | bytes 4194336 | tf_op jit(solution)/shard_map/ppermute | solution.py:456
  207.1 37.4 %attention.7.refs_7_ = bf16[2048,512]{1,0:T(8,128)(2,1)} custom-call(bf16[4096,768]{1,0:T(8,128)(2,1)} %convolution_convert_fusion.q_ref.kv_ref, bf16[4096,768]{1,0:T(8,128)(2,1)} %convolution_convert_fusion.q_ref.kv_ref, f32[2048,128]{1,0:T(8,128)} %copy.40.cos_ref, f32[2048,128]{1,0:T(8,128)} %copy.41.sin_ref, bf16[4096,128]{1,0:T(8,128)(2,1)} %select_convert_fusion.aug_ref), custom_call_target="tpu_custom_call" | custom-call | flops 17179869184 | bytes 10485760 | tf_op jit(solution)/shard_map/attention/pallas_call | solution.py:102
  244.5 7.3 collective-permute-done.9.refs_16_.refs_2_
  252.0 1.0 copy.53
  253.0 1.0 copy.54
  254.0 1.4 pad_maximum_fusion
  255.4 2.5 copy.52
  257.9 37.5 %attention.4.refs_1_ = bf16[2048,512]{1,0:T(8,128)(2,1)} custom-call(bf16[4096,768]{1,0:T(8,128)(2,1)} %convolution_convert_fusion.1.q_ref.kv_ref, bf16[4096,768]{1,0:T(8,128)(2,1)} %convolution_convert_fusion.1.q_ref.kv_ref, f32[2048,128]{1,0:T(8,128)} %copy.40.cos_ref, f32[2048,128]{1,0:T(8,128)} %copy.41.sin_ref, bf16[4096,128]{1,0:T(8,128)(2,1)} %select_convert_fusion.aug_ref), custom_call_target="tpu_custom_call" | custom-call | flops 17179869184 | bytes 10485760 | tf_op jit(solution)/shard_map/attention/pallas_call | solution.py:102
  295.4 1.6 collective-permute-start.1
  297.0 0.5 collective-permute-start.4
  297.5 1.5 collective-permute-start.2
  299.0 0.1 maximum_convert_fusion
  299.1 0.3 subtract_convert_fusion
  299.5 2.1 maximum_select_fusion.1
  301.6 7.1 place.3
  308.7 18.6 %place.2 = (bf16[2048,2048]{1,0:T(8,128)(2,1)}, bf16[2048,2048]{1,0:T(8,128)(2,1)}) custom-call(s32[1]{0:T(128)} %bitcast.9.base_ref, bf16[2048,1024]{1,0:T(8,128)(2,1)} %refs_0_, bf16[2048,1024]{1,0:T(8,128)(2,1)} %collective-permute-done.5.refs_11_.refs_1_, bf16[2048,1024]{1,0:T(8,128)(2,1)} %collective-permute-done.6.refs_12_.refs_2_, ...), custom_call_target="tpu_custom_call" | custom-call | flops 4294967296 | bytes 33554432 | tf_op jit(solution)/shard_map/place/pallas_call | solution.py:138
  327.3 3.2 constant_dynamic-slice_fusion
  330.4 58.8 %collective-permute-done.4.refs_8_ = bf16[2048,512]{1,0:T(8,128)(2,1)} collective-permute-done((bf16[2048,512]{1,0:T(8,128)(2,1)}, bf16[2048,512]{1,0:T(8,128)(2,1)}, u32[]{:S(2)}, u32[]{:S(2)}) %collective-permute-start.4) | collective-permute-done | bytes 2097184 | tf_op jit(solution)/shard_map/ppermute | solution.py:461
  389.2 44.5 %collective-permute-done.2.refs_4_ = bf16[2048,512]{1,0:T(8,128)(2,1)} collective-permute-done((bf16[2048,512]{1,0:T(8,128)(2,1)}, bf16[2048,512]{1,0:T(8,128)(2,1)}, u32[]{:S(2)}, u32[]{:S(2)}) %collective-permute-start.2) | collective-permute-done | bytes 2097184 | tf_op jit(solution)/shard_map/ppermute | solution.py:461
  433.7 434.6 %mlp.1 = (bf16[4096,2048]{1,0:T(8,128)(2,1)}, bf16[4096,2048]{1,0:T(8,128)(2,1)}, bf16[4096,2048]{1,0:T(8,128)(2,1)}) custom-call(bf16[4096,2048]{1,0:T(8,128)(2,1)} %bitcast.17, bf16[2048,512]{1,0:T(8,128)(2,1)} %attention.4.refs_1_, bf16[2048,512]{1,0:T(8,128)(2,1)} %collective-permute-done.1.refs_2_, bf16[2048,512]{1,0:T(8,128)(2,1)} %attention.5.refs_3_, ...), custom_call_target="tpu_custom_call" | custom-call | flops 137438953472 | bytes 67108864 | tf_op jit(solution)/shard_map/mlp/pallas_call | solution.py:402
  868.3 14.2 %copy.61 = bf16[2,2048,2048]{2,1,0:T(8,128)(2,1)} copy(bf16[2,2048,2048]{2,1,0:T(8,128)(2,1)} %bitcast.18) | data formatting | bytes 33554432
  (49 shorter events, 0.7 us)
Async XLA Ops:
  7.2 33.7 %all-gather.4.cloned.1.call-start = ((), (), s32[]{:S(2)}) async-start(), calls=%async_computation | async-start | bytes 3932160 | tf_op jit(solution)/shard_map/all_gather | solution.py:435
  7.9 11.5 %copy-start.9 = (bf16[2048]{0:T(1024)(128)(2,1)S(1)}, bf16[2048]{0:T(1024)(128)(2,1)}, u32[]{:S(2)}) copy-start(bf16[2048]{0:T(1024)(128)(2,1)} %param.18) | copy-start | bytes 12292
  7.9 117.8 %all-gather.6.cloned.1.call-start = ((), (), s32[]{:S(2)}) async-start(), calls=%async_computation.1 | async-start | bytes 3932160 | tf_op jit(solution)/shard_map/all_gather | solution.py:440
  8.0 52.9 %collective-permute-start = (bf16[2048,192]{0,1:T(8,128)(2,1)}, bf16[2048,192]{0,1:T(8,128)(2,1)S(1)}, u32[]{:S(2)}, u32[]{:S(2)}) collective-permute-start(bf16[2048,192]{0,1:T(8,128)(2,1)} %param.14), channel_id=1, source_target_pairs={{0,8},{8,0},{4,12},{12,4},{1,9},{9,1},{5,13},{13,5},{2,10},{10,2},... | collective-permute-start | bytes 2359304 | tf_op jit(solution)/shard_map/ppermute | solution.py:436
  60.8 0.9 copy-start.8
  61.7 265.5 %all-gather.8.cloned.1.call-start = ((), (), s32[]{:S(2)}) async-start(), calls=%async_computation.2 | async-start | bytes 8912896 | tf_op jit(solution)/shard_map/all_gather | solution.py:441
  63.5 0.7 copy-start
  63.5 3.6 copy-start.11
  63.5 3.7 copy-start.10
  70.9 136.2 %collective-permute-start.6 = (bf16[2048,1024]{1,0:T(8,128)(2,1)}, bf16[2048,1024]{1,0:T(8,128)(2,1)}, u32[]{:S(2)}, u32[]{:S(2)}) collective-permute-start(bf16[2048,1024]{1,0:T(8,128)(2,1)} %refs_0_), channel_id=1, source_target_pairs={{0,2},{2,0},{1,3},{3,1},{4,6},{6,4},{5,7},{7,5},{8,10},{10,8},{9,1... | collective-permute-start | bytes 12582920 | tf_op jit(solution)/shard_map/ppermute | solution.py:456
  71.3 225.7 %collective-permute-start.5 = (bf16[2048,1024]{1,0:T(8,128)(2,1)}, bf16[2048,1024]{1,0:T(8,128)(2,1)}, u32[]{:S(2)}, u32[]{:S(2)}) collective-permute-start(bf16[2048,1024]{1,0:T(8,128)(2,1)} %refs_0_), channel_id=1, source_target_pairs={{0,1},{1,0},{2,3},{3,2},{4,5},{5,4},{6,7},{7,6},{8,9},{9,8},{10,11... | collective-permute-start | bytes 12582920 | tf_op jit(solution)/shard_map/ppermute | solution.py:422
  71.3 180.6 %collective-permute-start.9 = (bf16[512,2048]{1,0:T(8,128)(2,1)}, bf16[512,2048]{1,0:T(8,128)(2,1)}, u32[]{:S(2)}, u32[]{:S(2)}) collective-permute-start(bf16[512,2048]{1,0:T(8,128)(2,1)} %refs_0_.1), channel_id=1, source_target_pairs={{0,2},{2,0},{1,3},{3,1},{4,6},{6,4},{5,7},{7,5},{8,10},{10,8},{9,1... | collective-permute-start | bytes 6291464 | tf_op jit(solution)/shard_map/ppermute | solution.py:457
  73.0 222.4 %collective-permute-start.8 = (bf16[512,2048]{1,0:T(8,128)(2,1)}, bf16[512,2048]{1,0:T(8,128)(2,1)}, u32[]{:S(2)}, u32[]{:S(2)}) collective-permute-start(bf16[512,2048]{1,0:T(8,128)(2,1)} %refs_0_.1), channel_id=1, source_target_pairs={{0,1},{1,0},{2,3},{3,2},{4,5},{5,4},{6,7},{7,6},{8,9},{9,8},{10,11... | collective-permute-start | bytes 6291464 | tf_op jit(solution)/shard_map/ppermute | solution.py:422
  110.4 278.9 %collective-permute-start.3 = (bf16[2048,512]{1,0:T(8,128)(2,1)}, bf16[2048,512]{1,0:T(8,128)(2,1)}, u32[]{:S(2)}, u32[]{:S(2)}) collective-permute-start(bf16[2048,512]{1,0:T(8,128)(2,1)} %attention.6.refs_5_), channel_id=1, source_target_pairs={{0,4},{4,0},{8,12},{12,8},{1,5},{5,1},{9,13},{13,9},{2,6},{6,2},{1... | collective-permute-start | bytes 6291464 | tf_op jit(solution)/shard_map/ppermute | solution.py:458
  207.1 101.6 %collective-permute-start.7 = (bf16[2048,1024]{1,0:T(8,128)(2,1)}, bf16[2048,1024]{1,0:T(8,128)(2,1)}, u32[]{:S(2)}, u32[]{:S(2)}) collective-permute-start(bf16[2048,1024]{1,0:T(8,128)(2,1)} %collective-permute-done.6.refs_12_.refs_2_), channel_id=1, source_target_pairs={{0,1},{1,0},{2,3},{3,2},{4,5},{5,4},{6,7},{7,6},{8,9},{9,8},{10,11... | collective-permute-start | bytes 12582920 | tf_op jit(solution)/shard_map/ppermute | solution.py:422
  251.9 45.6 %collective-permute-start.10 = (bf16[512,2048]{1,0:T(8,128)(2,1)}, bf16[512,2048]{1,0:T(8,128)(2,1)}, u32[]{:S(2)}, u32[]{:S(2)}) collective-permute-start(bf16[512,2048]{1,0:T(8,128)(2,1)} %collective-permute-done.9.refs_16_.refs_2_), channel_id=1, source_target_pairs={{0,1},{1,0},{2,3},{3,2},{4,5},{5,4},{6,7},{7,6},{8,9},{9,8},{10,11... | collective-permute-start | bytes 6291464 | tf_op jit(solution)/shard_map/ppermute | solution.py:422
  257.9 41.1 %copy-start.4 = (bf16[2,2048,64]{1,2,0:T(8,128)(2,1)S(1)}, bf16[2,2048,64]{1,2,0:T(8,128)(2,1)}, u32[]{:S(2)}) copy-start(bf16[2,2048,64]{1,2,0:T(8,128)(2,1)} %copy.55) | copy-start | bytes 1572868
  257.9 41.1 %copy-start.5 = (bf16[2,2048,64]{1,2,0:T(8,128)(2,1)S(1)}, bf16[2,2048,64]{1,2,0:T(8,128)(2,1)}, u32[]{:S(2)}) copy-start(bf16[2,2048,64]{1,2,0:T(8,128)(2,1)} %copy.56) | copy-start | bytes 1572868
  257.9 41.3 %copy-start.1 = (f32[2048,32]{0,1:T(8,128)S(1)}, f32[2048,32]{0,1:T(8,128)}, u32[]{:S(2)}) copy-start(f32[2048,32]{0,1:T(8,128)} %copy-done) | copy-start | bytes 786436
  295.4 4.1 copy-start.2
  295.4 4.1 copy-start.3
  295.4 4.1 copy-start.6
  295.4 4.1 copy-start.7
  295.4 93.8 %collective-permute-start.1 = (bf16[2048,512]{1,0:T(8,128)(2,1)}, bf16[2048,512]{1,0:T(8,128)(2,1)}, u32[]{:S(2)}, u32[]{:S(2)}) collective-permute-start(bf16[2048,512]{1,0:T(8,128)(2,1)} %attention.4.refs_1_), channel_id=1, source_target_pairs={{0,4},{4,0},{8,12},{12,8},{1,5},{5,1},{9,13},{13,9},{2,6},{6,2},{1... | collective-permute-start | bytes 6291464 | tf_op jit(solution)/shard_map/ppermute | solution.py:458
  297.0 92.3 %collective-permute-start.4 = (bf16[2048,512]{1,0:T(8,128)(2,1)}, bf16[2048,512]{1,0:T(8,128)(2,1)}, u32[]{:S(2)}, u32[]{:S(2)}) collective-permute-start(bf16[2048,512]{1,0:T(8,128)(2,1)} %attention.7.refs_7_), channel_id=1, source_target_pairs={{0,4},{4,0},{8,12},{12,8},{1,5},{5,1},{9,13},{13,9},{2,6},{6,2},{1... | collective-permute-start | bytes 6291464 | tf_op jit(solution)/shard_map/ppermute | solution.py:461
  297.5 136.2 %collective-permute-start.2 = (bf16[2048,512]{1,0:T(8,128)(2,1)}, bf16[2048,512]{1,0:T(8,128)(2,1)}, u32[]{:S(2)}, u32[]{:S(2)}) collective-permute-start(bf16[2048,512]{1,0:T(8,128)(2,1)} %attention.5.refs_3_), channel_id=1, source_target_pairs={{0,4},{4,0},{8,12},{12,8},{1,5},{5,1},{9,13},{13,9},{2,6},{6,2},{1... | collective-permute-start | bytes 6291464 | tf_op jit(solution)/shard_map/ppermute | solution.py:461
Sparse Core Ops, SparseCore 0:
  9.5 31.2 all-gather.3
  61.9 43.3 all-gather.5
  107.4 114.1 all-gather.7
where the time goes:
time: 898 us; the launch traced here: 889 us
  Pallas kernels  610 us (68%)
  waiting for transfers between devices  157 us (17%)
  local copies, waits for them, and re-layouts  40.7 us (5%)
  matrix products  40.4 us (4%)
  other arithmetic  15.6 us (2%)
  between operations  14.5 us (2%)
  starting transfers between devices  11.6 us (1%)
    pallas_call x1, Pallas kernels, mlp(): pl.pallas_call(functools.partial(mlp_kernel, chunk, batch), in_specs=[any...  435 us
    pallas_call x4, Pallas kernels, attention(): pl.pallas_call(functools.partial(attn_kernel, tile), grid=(groups, 2), in...  149 us
    ppermute x2, waiting for transfers between devices, layer(): near_far.append(lax.ppermute(heads_far[b], 'tpa', NEAR_ROW))  103 us
    dot_general x2, matrix products, dot(): return jnp.dot(a, b, preferred_element_type=jnp.float32)  40.4 us
    unnamed x33, local copies, waits for them, and re-layouts  26.2 us
    pallas_call x2, Pallas kernels, place(): pl.pallas_call(place_kernel, grid_spec=pltpu.PrefetchScalarGridSpec(num_s...  25.7 us
    ppermute x1, waiting for transfers between devices, layer(): gu_chip = lax.ppermute(w_gate_up, 'tpb', OTHER_CHIP)  23.7 us
    all_gather x1, waiting for transfers between devices, layer(): qkv_own = lax.all_gather(w_qkv, 'tpb', axis=1, tiled=True)  21.4 us
  transfers between devices with their start and end apart: 14, of which 5 were waited for; matrix products, arithmetic and copies ran while one was open for 9% of the time, Pallas kernels for 20%

commit v1 on v0

--- a/solution.py
+++ b/solution.py
@@ -150,13 +150,11 @@
     (wo_ref, ga_ref, gb_ref, gc_ref, gd_ref, da_ref, db_ref, dc_ref, dd_ref, gain_ref,
      y_ref, land_in, land_across,
      wo_v, gu_v, down_v, x_v, o_v, h_v, u_v, acc_v, part_v, half_v, stage_v, y_v,
-     w_sem, in_sem, stage_sem, in_send, in_recv, ac_send, ac_recv, out_send, out_recv, y_sem, tail_sem) = refs
+     w_sem, in_sem, stage_sem, in_send, in_recv, ac_send, ac_recv, out_send, out_recv, y_sem) = refs
     rows_all, _ = x_ref.shape
     count = rows_all // chunk
     heads = heads_refs[0].shape[1]
     per_prompt = count // batch
-    last = count - 1
-    half_rows = chunk // 2
     ff = da_ref.shape[0]
     part_id = lax.axis_index('part')
     z = lax.axis_index('tpa')
@@ -207,7 +205,11 @@
                 for copy in input_copies(k, prompt):
                     copy.start()
 
-    weights = [pltpu.make_async_copy(wo_ref, wo_v, w_sem.at[8])]
+    o_rows = wo_ref.shape[2]
+    weights = []
+    for t in range(4):
+        for row in range(4):
+            weights.append(pltpu.make_async_copy(wo_ref.at[t, row], wo_v.at[pl.ds((4 * row + t) * o_rows, o_rows)], w_sem.at[8 + 4 * t + row]))
     for n, (g_ref, d_ref) in enumerate(((ga_ref, da_ref), (gb_ref, db_ref), (gc_ref, dc_ref), (gd_ref, dd_ref))):
         weights.append(pltpu.make_async_copy(g_ref, gu_v.at[n], w_sem.at[2 * n]))
         weights.append(pltpu.make_async_copy(d_ref, down_v.at[n], w_sem.at[2 * n + 1]))
@@ -226,31 +228,23 @@
     def keep_out(k):
         return pltpu.make_async_copy(y_v.at[k % 2], y_ref.at[rows_of(k)], y_sem.at[k % 2])
 
-    def tail(ref, n):
-        return ref.at[pl.ds(last * chunk + n * half_rows, half_rows)]
-
-    def tail_copy(src, dst, row, which, n):
-        return pltpu.make_async_remote_copy(src_ref=src.at[:, pl.ds(n * half_rows, half_rows)].at[0], dst_ref=tail(dst, n), send_sem=tail_sem.at[which, n], recv_sem=tail_sem.at[which + 1, n], device_id=device(row), device_id_type=mesh_ids)
-
-    def tail_in(n):
-        return tail_copy(part_v.at[pl.ds(last % 3, 1)], land_in, inner, 0, n)
-
-    def tail_across(n):
-        return tail_copy(half_v.at[pl.ds(last % 3, 1)], land_across, other, 2, n)
-
-    def tail_out(n):
-        return tail_copy(y_v.at[pl.ds(last % 2, 1)], y_ref, outer, 4, n)
-
-    def tail_keep(n):
-        return pltpu.make_async_copy(y_v.at[last % 2, pl.ds(n * half_rows, half_rows)], tail(y_ref, n), tail_sem.at[6, n])
-
-    def tail_fetch(ref, slot, n):
-        return pltpu.make_async_copy(tail(ref, n), stage_v.at[slot, pl.ds(n * half_rows, half_rows)], tail_sem.at[7, n])
-
     def fetch(ref, k, slot):
         return pltpu.make_async_copy(ref.at[rows_of(k)], stage_v.at[slot], stage_sem.at[slot])
 
     def step(k, carry):
+        takes_in = is_mid & (k >= 2) & (k < count + 2)
+        takes_across = is_mid & (k >= 4)
+
+        @pl.when(takes_in)
+        def _():
+            send_in(k - 2).wait_recv()
+            fetch(land_in, k - 2, 0).start()
+
+        @pl.when(takes_across)
+        def _():
+            send_across(k - 4).wait_recv()
+            fetch(land_across, k - 4, 1).start()
+
         @pl.when(k < count)
         def _():
             for copy in input_copies(k, 0):
@@ -262,7 +256,8 @@
 
             @pl.when(k == 0)
             def _():
-                weights[0].wait()
+                for copy in weights[:16]:
+                    copy.wait()
 
             @pl.when(is_end & (k >= 3))
             def _():
@@ -270,7 +265,7 @@
 
             slot = k % 2
             hidden = (x_v[slot].astype(jnp.float32) + jnp.dot(o_v[slot], wo_v[...], preferred_element_type=jnp.float32)).astype(jnp.bfloat16)
-            h_v[k % 3] = hidden
+            h_v[k % 5] = hidden
             wide = hidden.astype(jnp.float32)
             mean_sq = jnp.mean(wide * wide, axis=1, keepdims=True)
             u_v[...] = (wide * lax.rsqrt(mean_sq + NORM_EPS) * gain_ref[...].astype(jnp.float32)).astype(jnp.bfloat16)
@@ -292,103 +287,59 @@
             lax.fori_loop(0, 4, ff_block, 0)
             part_v[k % 3] = acc_v[...].astype(jnp.bfloat16)
 
-            @pl.when(is_end & (k < last))
+            @pl.when(is_end)
             def _():
                 send_in(k).start()
 
-            @pl.when(is_end & (k == last))
-            def _():
-                for n in range(2):
-                    tail_in(n).start()
-
-        @pl.when(is_mid & (k >= 1) & (k < count))
+        @pl.when(takes_in)
         def _():
-            j = k - 1
-            send_in(j).wait_recv()
-            copy = fetch(land_in, j, 0)
-            copy.start()
+            j = k - 2
 
             @pl.when(j >= 3)
             def _():
                 send_across(j - 3).wait_send()
 
-            copy.wait()
+            fetch(land_in, j, 0).wait()
             half_v[j % 3] = (part_v[j % 3].astype(jnp.float32) + stage_v[0].astype(jnp.float32)).astype(jnp.bfloat16)
             send_across(j).start()
 
-        @pl.when(is_mid & (k == count))
+        @pl.when(takes_across)
         def _():
-            send_across(last - 3).wait_send()
-            for n in range(2):
-                tail_in(n).wait_recv()
-                copy = tail_fetch(land_in, 0, n)
-                copy.start()
-                copy.wait()
-                rows = slice(n * half_rows, (n + 1) * half_rows)
-                half_v[last % 3, rows, :] = (part_v[last % 3, rows, :].astype(jnp.float32) + stage_v[0, rows, :].astype(jnp.float32)).astype(jnp.bfloat16)
-                tail_across(n).start()
-
-        @pl.when(is_mid & (k >= 2) & (k <= count))
-        def _():
-            j = k - 2
-            send_across(j).wait_recv()
-            copy = fetch(land_across, j, 1)
-            copy.start()
+            j = k - 4
 
             @pl.when(j >= 2)
             def _():
                 send_out(j - 2).wait_send()
                 keep_out(j - 2).wait()
 
-            copy.wait()
+            fetch(land_across, j, 1).wait()
             total = half_v[j % 3].astype(jnp.float32) + stage_v[1].astype(jnp.float32)
-            y_v[j % 2] = (h_v[j % 3].astype(jnp.float32) + total).astype(jnp.bfloat16)
+            y_v[j % 2] = (h_v[j % 5].astype(jnp.float32) + total).astype(jnp.bfloat16)
             send_out(j).start()
             keep_out(j).start()
 
-        @pl.when(is_mid & (k > count))
-        def _():
-            send_out(last - 2).wait_send()
-            keep_out(last - 2).wait()
-            for n in range(2):
-                tail_across(n).wait_recv()
-                copy = tail_fetch(land_across, 1, n)
-                copy.start()
-                copy.wait()
-                rows = slice(n * half_rows, (n + 1) * half_rows)
-                total = half_v[last % 3, rows, :].astype(jnp.float32) + stage_v[1, rows, :].astype(jnp.float32)
-                y_v[last % 2, rows, :] = (h_v[last % 3, rows, :].astype(jnp.float32) + total).astype(jnp.bfloat16)
-                tail_out(n).start()
-                tail_keep(n).start()
-
         return carry
 
-    lax.fori_loop(0, count + 2, step, 0)
+    lax.fori_loop(0, count + 4, step, 0)
 
     @pl.when(is_end)
     def _():
-        for k in range(count - 3, last):
+        for k in range(count - 3, count):
             send_in(k).wait_send()
 
         def arrive(k, carry):
             send_out(k).wait_recv()
             return carry
 
-        lax.fori_loop(0, last, arrive, 0)
-        for n in range(2):
-            tail_in(n).wait_send()
-            tail_out(n).wait_recv()
+        lax.fori_loop(0, count, arrive, 0)
 
     @pl.when(is_mid)
     def _():
-        for k in range(count - 3, last):
+        for k in range(count - 3, count):
             send_across(k).wait_send()
-        send_out(last - 1).wait_send()
-        keep_out(last - 1).wait()
-        for n in range(2):
-            tail_across(n).wait_send()
-            tail_out(n).wait_send()
-            tail_keep(n).wait()
+        for k in range(count - 2, count):
+            send_out(k).wait_send()
+            keep_out(k).wait()
 
 
 def mlp(x_flat, heads, w_o_all, gu, down, gain, chunk, batch):
@@ -397,7 +348,7 @@
     ff = down[0].shape[0]
     anywhere = pl.BlockSpec(memory_space=pl.ANY)
     whole = jax.ShapeDtypeStruct((rows, dim), jnp.bfloat16)
-    inner = w_o_all.shape[0]
+    inner = w_o_all.shape[0] * w_o_all.shape[1] * w_o_all.shape[2]
     dma = pltpu.SemaphoreType.DMA
     out = pl.pallas_call(
         functools.partial(mlp_kernel, chunk, batch),
@@ -406,10 +357,10 @@
         out_shape=[whole] * 3,
         scratch_shapes=[
             pltpu.VMEM((inner, dim), jnp.bfloat16), pltpu.VMEM((4, dim, 2 * ff), jnp.bfloat16), pltpu.VMEM((4, ff, dim), jnp.bfloat16),
-            pltpu.VMEM((2, chunk, dim), jnp.bfloat16), pltpu.VMEM((2, chunk, inner), jnp.bfloat16), pltpu.VMEM((3, chunk, dim), jnp.bfloat16),
+            pltpu.VMEM((2, chunk, dim), jnp.bfloat16), pltpu.VMEM((2, chunk, inner), jnp.bfloat16), pltpu.VMEM((5, chunk, dim), jnp.bfloat16),
             pltpu.VMEM((chunk, dim), jnp.bfloat16), pltpu.VMEM((chunk, dim), jnp.float32), pltpu.VMEM((3, chunk, dim), jnp.bfloat16),
             pltpu.VMEM((3, chunk, dim), jnp.bfloat16), pltpu.VMEM((2, chunk, dim), jnp.bfloat16), pltpu.VMEM((2, chunk, dim), jnp.bfloat16),
-            dma((9,)), dma((2, 5)), dma((2,)), dma((count,)), dma((count,)), dma((count,)), dma((count,)), dma((count,)), dma((count,)), dma((2,)), dma((8, 2)),
+            dma((24,)), dma((2, 5)), dma((2,)), dma((count,)), dma((count,)), dma((count,)), dma((count,)), dma((count,)), dma((count,)), dma((2,)),
         ],
         compiler_params=pltpu.CompilerParams(collective_id=1, has_side_effects=True, vmem_limit_bytes=63 * 1024 * 1024),
         cost_estimate=pl.CostEstimate(flops=2 * rows * dim * (inner + 12 * ff), bytes_accessed=8 * rows * dim, transcendentals=4 * rows * ff),
@@ -438,7 +389,7 @@
     act_own = dot(normed, qkv_own).astype(jnp.bfloat16)
     act_own, far = lax.optimization_barrier((act_own, far))
     qkv_far = lax.all_gather(far, 'tpb', axis=1, tiled=True)
-    w_o_all = lax.all_gather(w_o, ('tpa', 'tpb'), axis=0, tiled=True)
+    w_o_all = lax.all_gather(lax.all_gather(w_o, 'tpa', axis=0), 'tpb', axis=0)
     w_gate_up, w_down, _ = lax.optimization_barrier((w_gate_up, w_down, qkv_own))
     cos_tab, sin_tab = rope_tables(seq, HEAD)
     cos_wide = jnp.tile(cos_tab, (1, 4))
@@ -469,8 +420,7 @@
     heads = []
     for b in range(batch):
         heads += [heads_own[b], near_own[b], heads_far[b], near_far[b]]
-    o_rows = w_o_all.shape[0] // 4
-    w_o_gen = lax.dynamic_slice(w_o_all, (tpa * o_rows, 0), (o_rows, w_o_all.shape[1]))
+    w_o_gen = lax.dynamic_index_in_dim(w_o_all, tpa, 1, keepdims=False).reshape(4 * w_o.shape[0], w_o.shape[1])
     heads[-1], w_o_gen = lax.optimization_barrier((heads[-1], w_o_gen))
     layer_out = mlp(x_flat, heads, w_o_all, gu, down, g_mlp, min(256, seq // 8), batch).reshape(batch, seq, model_dim)
 

time: 898 us -> 962 us (1.071)
  waiting for transfers between devices: 157 us -> 194 us
  Pallas kernels: 610 us -> 640 us
    pallas_call x1, Pallas kernels: 435 us -> 464 us  [mlp(): pl.pallas_call(functools.partial(mlp_kernel, chunk, batch), in_specs=[any...]
    ppermute x1, waiting for transfers between devices: 23.7 us -> 42.8 us  [layer(): gu_chip = lax.ppermute(w_gate_up, 'tpb', OTHER_CHIP)]
    all_gather x1 -> x2, waiting for transfers between devices: 0.01 us -> 17.9 us  [layer(): w_o_all = lax.all_gather(lax.all_gather(w_o, 'tpa', axis=0), 'tpb', axis=0)]
  transfers between devices with their start and end apart: 14 -> 15, of which waited for: 5 -> 6; matrix products, arithmetic and copies ran while one was open for 9% -> 9% of each run, Pallas kernels for 20% -> 18%
where the time goes in v1:
time: 962 us; the launch traced here: 955 us
  Pallas kernels  640 us (67%)
  waiting for transfers between devices  194 us (20%)
  matrix products  42.1 us (4%)
  local copies, waits for them, and re-layouts  40.6 us (4%)
  other arithmetic  15.7 us (2%)
  between operations  14.5 us (2%)
    pallas_call x1, Pallas kernels, mlp(): pl.pallas_call(functools.partial(mlp_kernel, chunk, batch), in_specs=[any...  464 us
    pallas_call x4, Pallas kernels, attention(): pl.pallas_call(functools.partial(attn_kernel, tile), grid=(groups, 2), in...  149 us
    ppermute x2, waiting for transfers between devices, layer(): near_far.append(lax.ppermute(heads_far[b], 'tpa', NEAR_ROW))  105 us
    ppermute x1, waiting for transfers between devices, layer(): gu_chip = lax.ppermute(w_gate_up, 'tpb', OTHER_CHIP)  42.8 us
    dot_general x2, matrix products, dot(): return jnp.dot(a, b, preferred_element_type=jnp.float32)  42.1 us
    unnamed x33, local copies, waits for them, and re-layouts  26.1 us
    pallas_call x2, Pallas kernels, place(): pl.pallas_call(place_kernel, grid_spec=pltpu.PrefetchScalarGridSpec(num_s...  25.7 us
    all_gather x1, waiting for transfers between devices, layer(): qkv_own = lax.all_gather(w_qkv, 'tpb', axis=1, tiled=True)  21.2 us
  transfers between devices with their start and end apart: 15, of which 6 were waited for; matrix products, arithmetic and copies ran while one was open for 9% of the time, Pallas kernels for 18%

profile of v1, /device:TPU:0, one launch (start us, length us, event | category | flops | bytes accessed | tf_op | source)
XLA Modules:
  0.0 954.9 jit_solution(16170179322698270386)
XLA Ops:
  7.2 0.7 all-gather.7.cloned.1.call-update
  8.0 4.1 collective-permute-start
  12.2 7.4 multiply_reduce_fusion
  19.6 21.2 %all-gather.7.cloned.1.call-done = bf16[2048,768]{0,1:T(8,128)(2,1)} async-done(((bf16[2048,192]{0,1:T(8,128)(2,1)}), bf16[2048,768]{0,1:T(8,128)(2,1)}) %all-gather.7.cloned.1.call-update) | async-done | bytes 3145744 | tf_op jit(solution)/shard_map/all_gather | solution.py:386
  40.8 20.0 %convolution_convert_fusion.1.q_ref.kv_ref = bf16[4096,768]{1,0:T(8,128)(2,1)} fusion(bf16[2048,768]{0,1:T(8,128)(2,1)} %all-gather.7.cloned.1.call-done, bf16[4096,2048]{1,0:T(8,128)(2,1)} %bitcast.18, f32[2048]{0:T(1024)S(1)} %convert_element_type.28, f32[4096]{0:T(1024)S(1)} %bitcast.33), kind=kOutput, calls=%fused_computation.3 | convolution fusion | flops 12921602048 | bytes 26238976 | tf_op jit(solution)/shard_map/dot_general | solution.py:377
  60.8 0.9 copy-done.8
  61.8 1.0 fusion.2
  62.8 0.7 copy-done
  63.6 0.1 tile.32
  63.7 1.3 copy.41.sin_ref
  65.1 1.3 copy.40.cos_ref
  66.5 0.6 reshape.175.refs_18_
  67.1 3.1 select_convert_fusion.aug_ref
  70.2 17.9 %all-gather.11.cloned.1.call-done = bf16[512,2048]{1,0:T(8,128)(2,1)} async-done(((bf16[128,2048]{1,0:T(8,128)(2,1)}), bf16[512,2048]{1,0:T(8,128)(2,1)}) %all-gather.11.cloned.1.call-update) | async-done | bytes 2097168 | tf_op jit(solution)/shard_map/all_gather | solution.py:392
  88.1 1.5 collective-permute-start.6
  89.6 0.6 collective-permute-start.9
  90.2 0.2 collective-permute-start.8
  90.4 37.2 %attention.6.refs_5_ = bf16[2048,512]{1,0:T(8,128)(2,1)} custom-call(bf16[4096,768]{1,0:T(8,128)(2,1)} %convolution_convert_fusion.1.q_ref.kv_ref, bf16[4096,768]{1,0:T(8,128)(2,1)} %convolution_convert_fusion.1.q_ref.kv_ref, f32[2048,128]{1,0:T(8,128)} %copy.40.cos_ref, f32[2048,128]{1,0:T(8,128)} %copy.41.sin_ref, bf16[4096,128]{1,0:T(8,128)(2,1)} %select_convert_fusion.aug_ref), custom_call_target="tpu_custom_call" | custom-call | flops 17179869184 | bytes 10485760 | tf_op jit(solution)/shard_map/attention/pallas_call | solution.py:102
  127.6 0.2 collective-permute-start.3
  127.8 4.0 fusion.3
  131.8 2.3 copy.55
  134.1 1.1 copy.56
  135.2 1.2 copy.57
  136.4 1.1 copy.58
  137.5 1.3 fusion.4
  138.8 2.7 fusion.5
  141.5 22.1 %convolution_convert_fusion.q_ref.kv_ref = bf16[4096,768]{1,0:T(8,128)(2,1)} fusion(bf16[2048,768]{0,1:T(8,128)(2,1)} %all-gather.9.cloned.1.call-done, bf16[4096,2048]{1,0:T(8,128)(2,1)} %bitcast.19, f32[2048]{0:T(1024)S(1)} %convert_element_type.28, f32[4096]{0:T(1024)S(1)} %bitcast.34), kind=kOutput, calls=%fused_computation.2 | convolution fusion | flops 12921602048 | bytes 26238976 | tf_op jit(solution)/shard_map/dot_general | solution.py:377
  163.6 37.3 %attention.5.refs_3_ = bf16[2048,512]{1,0:T(8,128)(2,1)} custom-call(bf16[4096,768]{1,0:T(8,128)(2,1)} %convolution_convert_fusion.q_ref.kv_ref, bf16[4096,768]{1,0:T(8,128)(2,1)} %convolution_convert_fusion.q_ref.kv_ref, f32[2048,128]{1,0:T(8,128)} %copy.40.cos_ref, f32[2048,128]{1,0:T(8,128)} %copy.41.sin_ref, bf16[4096,128]{1,0:T(8,128)(2,1)} %select_convert_fusion.aug_ref), custom_call_target="tpu_custom_call" | custom-call | flops 17179869184 | bytes 10485760 | tf_op jit(solution)/shard_map/attention/pallas_call | solution.py:102
  200.9 42.8 %collective-permute-done.6.refs_12_.refs_2_ = bf16[2048,1024]{1,0:T(8,128)(2,1)} collective-permute-done((bf16[2048,1024]{1,0:T(8,128)(2,1)}, bf16[2048,1024]{1,0:T(8,128)(2,1)}, u32[]{:S(2)}, u32[]{:S(2)}) %collective-permute-start.6) | collective-permute-done | bytes 4194336 | tf_op jit(solution)/shard_map/ppermute | solution.py:407
  243.7 37.4 %attention.7.refs_7_ = bf16[2048,512]{1,0:T(8,128)(2,1)} custom-call(bf16[4096,768]{1,0:T(8,128)(2,1)} %convolution_convert_fusion.q_ref.kv_ref, bf16[4096,768]{1,0:T(8,128)(2,1)} %convolution_convert_fusion.q_ref.kv_ref, f32[2048,128]{1,0:T(8,128)} %copy.40.cos_ref, f32[2048,128]{1,0:T(8,128)} %copy.41.sin_ref, bf16[4096,128]{1,0:T(8,128)(2,1)} %select_convert_fusion.aug_ref), custom_call_target="tpu_custom_call" | custom-call | flops 17179869184 | bytes 10485760 | tf_op jit(solution)/shard_map/attention/pallas_call | solution.py:102
  281.1 6.2 collective-permute-done.9.refs_16_.refs_2_
  287.4 0.1 pad_maximum_fusion.2
  287.5 1.0 copy.53
  288.5 1.0 copy.54
  289.5 1.4 pad_maximum_fusion
  290.9 2.5 copy.52
  293.4 37.5 %attention.4.refs_1_ = bf16[2048,512]{1,0:T(8,128)(2,1)} custom-call(bf16[4096,768]{1,0:T(8,128)(2,1)} %convolution_convert_fusion.1.q_ref.kv_ref, bf16[4096,768]{1,0:T(8,128)(2,1)} %convolution_convert_fusion.1.q_ref.kv_ref, f32[2048,128]{1,0:T(8,128)} %copy.40.cos_ref, f32[2048,128]{1,0:T(8,128)} %copy.41.sin_ref, bf16[4096,128]{1,0:T(8,128)(2,1)} %select_convert_fusion.aug_ref), custom_call_target="tpu_custom_call" | custom-call | flops 17179869184 | bytes 10485760 | tf_op jit(solution)/shard_map/attention/pallas_call | solution.py:102
  331.0 2.0 collective-permute-start.4
  333.1 0.1 maximum_convert_fusion
  333.2 0.3 subtract_convert_fusion
  333.6 2.1 maximum_select_fusion.1
  335.7 7.1 place.3
  342.8 18.6 %place.2 = (bf16[2048,2048]{1,0:T(8,128)(2,1)}, bf16[2048,2048]{1,0:T(8,128)(2,1)}) custom-call(s32[1]{0:T(128)} %bitcast.12.base_ref, bf16[2048,1024]{1,0:T(8,128)(2,1)} %refs_0_, bf16[2048,1024]{1,0:T(8,128)(2,1)} %collective-permute-done.5.refs_11_.refs_1_, bf16[2048,1024]{1,0:T(8,128)(2,1)} %collective-permute-done.6.refs_12_.refs_2_, ...), custom_call_target="tpu_custom_call" | custom-call | flops 4294967296 | bytes 33554432 | tf_op jit(solution)/shard_map/place/pallas_call | solution.py:138
  361.4 3.2 constant_dynamic-slice_fusion
  364.5 60.2 %collective-permute-done.4.refs_8_ = bf16[2048,512]{1,0:T(8,128)(2,1)} collective-permute-done((bf16[2048,512]{1,0:T(8,128)(2,1)}, bf16[2048,512]{1,0:T(8,128)(2,1)}, u32[]{:S(2)}, u32[]{:S(2)}) %collective-permute-start.4) | collective-permute-done | bytes 2097184 | tf_op jit(solution)/shard_map/ppermute | solution.py:412
  424.7 44.5 %collective-permute-done.2.refs_4_ = bf16[2048,512]{1,0:T(8,128)(2,1)} collective-permute-done((bf16[2048,512]{1,0:T(8,128)(2,1)}, bf16[2048,512]{1,0:T(8,128)(2,1)}, u32[]{:S(2)}, u32[]{:S(2)}) %collective-permute-start.2) | collective-permute-done | bytes 2097184 | tf_op jit(solution)/shard_map/ppermute | solution.py:412
  469.2 464.5 %mlp.1 = (bf16[4096,2048]{1,0:T(8,128)(2,1)}, bf16[4096,2048]{1,0:T(8,128)(2,1)}, bf16[4096,2048]{1,0:T(8,128)(2,1)}) custom-call(bf16[4096,2048]{1,0:T(8,128)(2,1)} %bitcast.20, bf16[2048,512]{1,0:T(8,128)(2,1)} %attention.4.refs_1_, bf16[2048,512]{1,0:T(8,128)(2,1)} %collective-permute-done.1.refs_2_, bf16[2048,512]{1,0:T(8,128)(2,1)} %attention.5.refs_3_, ...), custom_call_target="tpu_custom_call" | custom-call | flops 137438953472 | bytes 67108864 | tf_op jit(solution)/shard_map/mlp/pallas_call | solution.py:353
  933.7 14.2 %copy.61 = bf16[2,2048,2048]{2,1,0:T(8,128)(2,1)} copy(bf16[2,2048,2048]{2,1,0:T(8,128)(2,1)} %bitcast.21) | data formatting | bytes 33554432
  (52 shorter events, 0.7 us)
Async XLA Ops:
  7.2 33.6 %all-gather.7.cloned.1.call-start = ((), (), s32[]{:S(2)}) async-start(), calls=%async_computation | async-start | bytes 3932160 | tf_op jit(solution)/shard_map/all_gather | solution.py:386
  7.9 80.2 %all-gather.11.cloned.1.call-start = ((), (), s32[]{:S(2)}) async-start(), calls=%async_computation.2 | async-start | bytes 2621440 | tf_op jit(solution)/shard_map/all_gather | solution.py:392
  8.0 52.8 %collective-permute-start = (bf16[2048,192]{0,1:T(8,128)(2,1)}, bf16[2048,192]{0,1:T(8,128)(2,1)S(1)}, u32[]{:S(2)}, u32[]{:S(2)}) collective-permute-start(bf16[2048,192]{0,1:T(8,128)(2,1)} %param.14), channel_id=1, source_target_pairs={{0,8},{8,0},{4,12},{12,4},{1,9},{9,1},{5,13},{13,5},{2,10},{10,2},... | collective-permute-start | bytes 2359304 | tf_op jit(solution)/shard_map/ppermute | solution.py:387
  12.1 7.5 copy-start.9
  12.1 129.4 %all-gather.9.cloned.1.call-start = ((), (), s32[]{:S(2)}) async-start(), calls=%async_computation.1 | async-start | bytes 3932160 | tf_op jit(solution)/shard_map/all_gather | solution.py:391
  60.8 0.9 copy-start.8
  61.7 299.7 %all-gather.13.cloned.1.call-start = ((), (), s32[]{:S(2)}) async-start(), calls=%async_computation.3 | async-start | bytes 10485760 | tf_op jit(solution)/shard_map/all_gather | solution.py:392
  62.8 0.7 copy-start
  62.8 3.6 copy-start.11
  62.8 3.7 copy-start.10
  88.1 155.6 %collective-permute-start.6 = (bf16[2048,1024]{1,0:T(8,128)(2,1)}, bf16[2048,1024]{1,0:T(8,128)(2,1)}, u32[]{:S(2)}, u32[]{:S(2)}) collective-permute-start(bf16[2048,1024]{1,0:T(8,128)(2,1)} %refs_0_), channel_id=1, source_target_pairs={{0,2},{2,0},{1,3},{3,1},{4,6},{6,4},{5,7},{7,5},{8,10},{10,8},{9,1... | collective-permute-start | bytes 12582920 | tf_op jit(solution)/shard_map/ppermute | solution.py:407
  89.6 241.4 %collective-permute-start.5 = (bf16[2048,1024]{1,0:T(8,128)(2,1)}, bf16[2048,1024]{1,0:T(8,128)(2,1)}, u32[]{:S(2)}, u32[]{:S(2)}) collective-permute-start(bf16[2048,1024]{1,0:T(8,128)(2,1)} %refs_0_), channel_id=1, source_target_pairs={{0,1},{1,0},{2,3},{3,2},{4,5},{5,4},{6,7},{7,6},{8,9},{9,8},{10,11... | collective-permute-start | bytes 12582920 | tf_op jit(solution)/shard_map/ppermute | solution.py:373
  89.6 197.7 %collective-permute-start.9 = (bf16[512,2048]{1,0:T(8,128)(2,1)}, bf16[512,2048]{1,0:T(8,128)(2,1)}, u32[]{:S(2)}, u32[]{:S(2)}) collective-permute-start(bf16[512,2048]{1,0:T(8,128)(2,1)} %refs_0_.1), channel_id=1, source_target_pairs={{0,2},{2,0},{1,3},{3,1},{4,6},{6,4},{5,7},{7,5},{8,10},{10,8},{9,1... | collective-permute-start | bytes 6291464 | tf_op jit(solution)/shard_map/ppermute | solution.py:408
  90.2 240.7 %collective-permute-start.8 = (bf16[512,2048]{1,0:T(8,128)(2,1)}, bf16[512,2048]{1,0:T(8,128)(2,1)}, u32[]{:S(2)}, u32[]{:S(2)}) collective-permute-start(bf16[512,2048]{1,0:T(8,128)(2,1)} %refs_0_.1), channel_id=1, source_target_pairs={{0,1},{1,0},{2,3},{3,2},{4,5},{5,4},{6,7},{7,6},{8,9},{9,8},{10,11... | collective-permute-start | bytes 6291464 | tf_op jit(solution)/shard_map/ppermute | solution.py:373
  127.6 297.1 %collective-permute-start.3 = (bf16[2048,512]{1,0:T(8,128)(2,1)}, bf16[2048,512]{1,0:T(8,128)(2,1)}, u32[]{:S(2)}, u32[]{:S(2)}) collective-permute-start(bf16[2048,512]{1,0:T(8,128)(2,1)} %attention.6.refs_5_), channel_id=1, source_target_pairs={{0,4},{4,0},{8,12},{12,8},{1,5},{5,1},{9,13},{13,9},{2,6},{6,2},{1... | collective-permute-start | bytes 6291464 | tf_op jit(solution)/shard_map/ppermute | solution.py:409
  243.7 99.1 %collective-permute-start.7 = (bf16[2048,1024]{1,0:T(8,128)(2,1)}, bf16[2048,1024]{1,0:T(8,128)(2,1)}, u32[]{:S(2)}, u32[]{:S(2)}) collective-permute-start(bf16[2048,1024]{1,0:T(8,128)(2,1)} %collective-permute-done.6.refs_12_.refs_2_), channel_id=1, source_target_pairs={{0,1},{1,0},{2,3},{3,2},{4,5},{5,4},{6,7},{7,6},{8,9},{9,8},{10,11... | collective-permute-start | bytes 12582920 | tf_op jit(solution)/shard_map/ppermute | solution.py:373
  287.4 45.6 %collective-permute-start.10 = (bf16[512,2048]{1,0:T(8,128)(2,1)}, bf16[512,2048]{1,0:T(8,128)(2,1)}, u32[]{:S(2)}, u32[]{:S(2)}) collective-permute-start(bf16[512,2048]{1,0:T(8,128)(2,1)} %collective-permute-done.9.refs_16_.refs_2_), channel_id=1, source_target_pairs={{0,1},{1,0},{2,3},{3,2},{4,5},{5,4},{6,7},{7,6},{8,9},{9,8},{10,11... | collective-permute-start | bytes 6291464 | tf_op jit(solution)/shard_map/ppermute | solution.py:373
  293.4 39.7 %copy-start.4 = (bf16[2,2048,64]{1,2,0:T(8,128)(2,1)S(1)}, bf16[2,2048,64]{1,2,0:T(8,128)(2,1)}, u32[]{:S(2)}) copy-start(bf16[2,2048,64]{1,2,0:T(8,128)(2,1)} %copy.55) | copy-start | bytes 1572868
  293.4 39.7 %copy-start.5 = (bf16[2,2048,64]{1,2,0:T(8,128)(2,1)S(1)}, bf16[2,2048,64]{1,2,0:T(8,128)(2,1)}, u32[]{:S(2)}) copy-start(bf16[2,2048,64]{1,2,0:T(8,128)(2,1)} %copy.56) | copy-start | bytes 1572868
  293.4 39.9 %copy-start.1 = (f32[2048,32]{0,1:T(8,128)S(1)}, f32[2048,32]{0,1:T(8,128)}, u32[]{:S(2)}) copy-start(f32[2048,32]{0,1:T(8,128)} %copy-done) | copy-start | bytes 786436
  330.9 2.7 copy-start.2
  330.9 2.7 copy-start.3
  330.9 2.7 copy-start.6
  330.9 2.7 copy-start.7
  330.9 93.8 %collective-permute-start.1 = (bf16[2048,512]{1,0:T(8,128)(2,1)}, bf16[2048,512]{1,0:T(8,128)(2,1)}, u32[]{:S(2)}, u32[]{:S(2)}) collective-permute-start(bf16[2048,512]{1,0:T(8,128)(2,1)} %attention.4.refs_1_), channel_id=1, source_target_pairs={{0,4},{4,0},{8,12},{12,8},{1,5},{5,1},{9,13},{13,9},{2,6},{6,2},{1... | collective-permute-start | bytes 6291464 | tf_op jit(solution)/shard_map/ppermute | solution.py:409
  331.0 93.7 %collective-permute-start.4 = (bf16[2048,512]{1,0:T(8,128)(2,1)}, bf16[2048,512]{1,0:T(8,128)(2,1)}, u32[]{:S(2)}, u32[]{:S(2)}) collective-permute-start(bf16[2048,512]{1,0:T(8,128)(2,1)} %attention.7.refs_7_), channel_id=1, source_target_pairs={{0,4},{4,0},{8,12},{12,8},{1,5},{5,1},{9,13},{13,9},{2,6},{6,2},{1... | collective-permute-start | bytes 6291464 | tf_op jit(solution)/shard_map/ppermute | solution.py:412
  333.0 136.2 %collective-permute-start.2 = (bf16[2048,512]{1,0:T(8,128)(2,1)}, bf16[2048,512]{1,0:T(8,128)(2,1)}, u32[]{:S(2)}, u32[]{:S(2)}) collective-permute-start(bf16[2048,512]{1,0:T(8,128)(2,1)} %attention.5.refs_3_), channel_id=1, source_target_pairs={{0,4},{4,0},{8,12},{12,8},{1,5},{5,1},{9,13},{13,9},{2,6},{6,2},{1... | collective-permute-start | bytes 6291464 | tf_op jit(solution)/shard_map/ppermute | solution.py:412
Sparse Core Ops, SparseCore 0:
  9.5 31.2 all-gather.6
  42.4 45.6 all-gather.10
  90.2 44.2 all-gather.8
  135.9 103.2 all-gather.12
